TPU v7x, 256 devices: a whole 4x4x8 slice. The times are simulated.
256 devices in a mesh: seq: 32 (over y, z), head: 8 (over x, core).
Axes of the slice: x: 4, y: 4, z: 8, core: 2. Of those that a mesh axis runs over, the one named last changes fastest.
Arguments:
- tokens: bfloat16 [2, 4096, 2560], P(None, 'seq', 'head'), may hold values from -6 to 6
- token_mix: float32 [5, 2560], replicated, may hold values from 0.05 to 0.95
- receptance: bfloat16 [2560, 2560], P(None, 'head'), may hold values from -0.125 to 0.125
- key_weight: bfloat16 [2560, 2560], P(None, 'head'), may hold values from -0.125 to 0.125
- value_weight: bfloat16 [2560, 2560], P(None, 'head'), may hold values from -0.125 to 0.125
- decay_base: float32 [2560], P('head'), may hold values from -12.5 to -1.9
- decay_down_matrix: bfloat16 [2560, 96], replicated, may hold values from -0.125 to 0.125
- decay_up_matrix: bfloat16 [96, 2560], P(None, 'head'), may hold values from -0.625 to 0.625
- learn_base: float32 [2560], P('head'), may hold values from -1.5 to 1.5
- learning_down_matrix: bfloat16 [2560, 96], replicated, may hold values from -0.125 to 0.125
- learning_up_matrix: bfloat16 [96, 2560], P(None, 'head'), may hold values from -0.625 to 0.625
- key_scale: float32 [2560], P('head'), may hold values from 0.25 to 1.75
- key_blend: float32 [2560], P('head'), may hold values from 0.2 to 1
- norm_gain: float32 [2560], P('head'), may hold values from 0.25 to 1.75
- norm_bias: float32 [2560], P('head'), may hold values from -3 to 3
- output_weight: bfloat16 [2560, 2560], P('head'), may hold values from -0.125 to 0.125
Outputs:
- mixed_out: bfloat16 [2, 4096, 2560], P(None, 'seq', 'head')
All inputs are finite; a program needn't handle non-finite values.
Results may differ from a plain program's by a relative error of at most 0.014.
Values may be sent and summed in bfloat16 or wider, within the bound.
No kernel may reach another device: no remote copies, remote signals or barrier semaphores. Data moves between devices by JAX's collectives and lax.ppermute only.
A program may use at most 128 MiB of HBM per device.

v0:
```python
import jax
import jax.numpy as jnp
from jax import lax
from jax.sharding import Mesh
from jax.sharding import PartitionSpec as P

HEAD_SIZE = 64
SPAN = 64
SEQ = ("seq_0", "seq_1")


def shifted(block, axis, distance):
    devices = range(lax.axis_size(axis))
    route = [(i - distance, i) for i in devices if i - distance in devices]
    return lax.ppermute(block, axis, route)


def gather_turned(arrays, axis, dims):
    turned = [jnp.moveaxis(a, dim, 0) for a, dim in zip(arrays, dims)]
    widths = [t[0].size for t in turned]
    both = jnp.concatenate([t.reshape(-1, w) for t, w in zip(turned, widths)], axis=1)
    out = lax.all_gather(both, axis, axis=0, tiled=True)
    tiles = jnp.split(out, [sum(widths[:k]) for k in range(1, len(widths))], axis=1)
    return tuple(
        (
            jnp.moveaxis(b.reshape(-1, *t.shape[1:]), 0, dim)
            for b, t, dim in zip(tiles, turned, dims)
        )
    )


def filled_with(value, identity):
    return jnp.broadcast_to(jnp.asarray(identity, value.dtype), value.shape)


def prefix_by_axis(value, axes, combine, identity):
    before = start = filled_with(value, identity)
    running = value
    for axis in reversed(axes):
        length, position = (lax.axis_size(axis), lax.axis_index(axis))
        pieces = lax.all_gather(running, axis)
        inside, running = (start, start)
        for k in range(length):
            passed = k < position
            running = combine(running, pieces[k])
            inside = jnp.where(passed, running, inside)
        before = combine(inside, before)
    return before


def joined_along(tiles, dim):
    dims = list(tiles.shape[1:])
    dims[dim] *= tiles.shape[0]
    return jnp.moveaxis(tiles, 0, dim).reshape(dims)


def from_everyone(value, axis):
    copies = jnp.broadcast_to(value, (lax.axis_size(axis), *value.shape))
    return lax.all_to_all(copies, axis, split_axis=0, concat_axis=0, tiled=True)


def gather_directly(value, axis, dim):
    return joined_along(from_everyone(value, axis), dim)


def matmul(left, right):
    return jnp.matmul(left, right)


def combine_maps(earlier, later):
    size = later.shape[-2]
    moving = later[..., size:]
    adding = later[..., :size]
    return matmul(moving, earlier) + jnp.concatenate([adding, jnp.zeros_like(adding)], axis=-1)


def lower_pairs(first, second, keep):
    products = jnp.einsum("abcti,abcsi->abcts", first, second)
    return jnp.where(keep, products, 0.0)


def body(
    tokens,
    token_mix,
    receptance,
    key_weight,
    value_weight,
    decay_base,
    decay_down_matrix,
    decay_up_matrix,
    learn_base,
    learning_down_matrix,
    learning_up_matrix,
    key_scale,
    key_blend,
    norm_gain,
    norm_bias,
    output_weight,
):
    seq_count, length, local_width = tokens.shape
    row_count = seq_count * length
    head_count = local_width // HEAD_SIZE
    boundary = shifted(tokens[:, length - 1 :, :], SEQ, 1)
    weights = (receptance, decay_down_matrix, key_weight, value_weight, learning_down_matrix)
    feature_piece, edge_piece = gather_turned((tokens, boundary), "head", (2, 2))
    extent = feature_piece.shape[2]
    current = feature_piece.astype(jnp.float32)
    earlier = jnp.concatenate([edge_piece, feature_piece[:, :-1, :]], axis=1).astype(jnp.float32)
    change = earlier - current
    result = []
    for term_index in range(5):
        blended = (
            (current + change * token_mix[term_index])
            .astype(jnp.bfloat16)
            .reshape(row_count, extent)
        )
        weight_rows = weights[term_index]
        result.append(jnp.dot(blended, weight_rows, preferred_element_type=jnp.float32))
    recept_out, decay_pre, key_raw, value_out, learn_pre = tuple(result)
    decay_hidden = jnp.tanh(decay_pre).astype(jnp.bfloat16)
    learn_hidden = learn_pre.astype(jnp.bfloat16)
    decay_arg = decay_base + jnp.dot(
        decay_hidden, decay_up_matrix, preferred_element_type=jnp.float32
    )
    log_decay = -jnp.exp(-jax.nn.softplus(-decay_arg) - 0.5)
    learn_rate = jax.nn.sigmoid(
        learn_base + jnp.dot(learn_hidden, learning_up_matrix, preferred_element_type=jnp.float32)
    )
    scaled = (key_raw * key_scale).reshape(row_count, head_count, HEAD_SIZE)
    unit_key = (
        scaled / jnp.sqrt(jnp.sum(scaled * scaled, axis=-1, keepdims=True) + 1e-06)
    ).reshape(row_count, local_width)
    key_final = key_raw * (1.0 + (learn_rate - 1.0) * key_blend)
    span_count = length // SPAN

    def arrange(values):
        return values.reshape(seq_count, span_count, SPAN, head_count, HEAD_SIZE).transpose(
            0, 3, 1, 2, 4
        )

    recept_c = arrange(recept_out)
    decay_c = arrange(log_decay)
    unit_c = arrange(unit_key)
    learn_c = arrange(learn_rate)
    key_c = arrange(key_final)
    value_c = arrange(value_out)
    alpha_c = -unit_c
    beta_c = unit_c * learn_c
    cumul = jnp.cumsum(decay_c, axis=3)
    before_c = cumul - decay_c
    middle = cumul[:, :, :, SPAN // 2 - 1 : SPAN // 2, :]
    ending = cumul[:, :, :, SPAN - 1 :, :]
    left_alpha = alpha_c * jnp.exp(before_c - middle)
    left_recept = recept_c * jnp.exp(cumul - middle)
    right_beta = beta_c * jnp.exp(middle - cumul)
    right_key = key_c * jnp.exp(middle - cumul)
    positions = jnp.arange(SPAN)
    strict = positions[:, None] > positions[None, :]
    within = positions[:, None] >= positions[None, :]
    lower_ab = lower_pairs(left_alpha, right_beta, strict)
    lower_ak = lower_pairs(left_alpha, right_key, strict)
    lower_rb = lower_pairs(left_recept, right_beta, within)
    lower_rk = lower_pairs(left_recept, right_key, within)
    identity = jnp.eye(SPAN, dtype=jnp.float32)
    inverse = identity + lower_ab
    power = lower_ab
    for level in range(SPAN.bit_length() - 2):
        power = matmul(power, power)
        inverse = inverse + matmul(power, inverse)
    gain_key = matmul(inverse, alpha_c * jnp.exp(before_c))
    gain_value = matmul(inverse, matmul(lower_ak, value_c))
    query_eff = recept_c * jnp.exp(cumul) + matmul(lower_rb, gain_key)
    local_out = matmul(lower_rb, gain_value) + matmul(lower_rk, value_c)
    beta_end = beta_c * jnp.exp(ending - cumul)
    key_end = key_c * jnp.exp(ending - cumul)
    head_eye = jnp.eye(HEAD_SIZE, dtype=jnp.float32)
    transition = jnp.einsum("abctj,abctk->abcjk", beta_end, gain_key)
    transition = transition + head_eye * jnp.swapaxes(jnp.exp(ending), -1, -2)
    increment = jnp.einsum("abctk,abctv->abckv", beta_end, gain_value)
    increment = increment + jnp.einsum("abctk,abctv->abckv", key_end, value_c)
    start_aug = jnp.broadcast_to(
        jnp.concatenate([jnp.zeros((HEAD_SIZE, HEAD_SIZE), jnp.float32), head_eye], axis=1),
        (seq_count, head_count, HEAD_SIZE, 2 * HEAD_SIZE),
    )

    def advance(carry, step_items):
        moving, adding = step_items
        following = matmul(moving, carry) + jnp.concatenate(
            [adding, jnp.zeros_like(adding)], axis=-1
        )
        return (following, carry)

    total, entries = lax.scan(
        advance, start_aug, (jnp.moveaxis(transition, 2, 0), jnp.moveaxis(increment, 2, 0))
    )
    prefix = prefix_by_axis(total, SEQ, combine_maps, start_aug)
    state_in = prefix[..., :HEAD_SIZE]
    span_state = entries[..., :HEAD_SIZE] + matmul(entries[..., HEAD_SIZE:], state_in)
    span_state = jnp.moveaxis(span_state, 0, 2)
    output_c = matmul(query_eff, span_state) + local_out
    wkv = output_c.transpose(0, 2, 3, 1, 4).reshape(row_count, head_count, HEAD_SIZE)
    centred = wkv - jnp.mean(wkv, axis=-1, keepdims=True)
    spread = jnp.mean(centred * centred, axis=-1, keepdims=True)
    normed = (centred / jnp.sqrt(spread + 0.00064)).reshape(
        row_count, local_width
    ) * norm_gain + norm_bias
    normed = normed.astype(jnp.bfloat16)
    own_columns = lax.all_to_all(output_weight, "head", split_axis=1, concat_axis=0, tiled=True)
    weight_rows = own_columns
    result = jnp.dot(
        gather_directly(normed, "head", 1), weight_rows, preferred_element_type=jnp.float32
    )
    return result.astype(jnp.bfloat16).reshape(seq_count, length, local_width)


def solution(mesh):
    torus = Mesh(mesh.devices.reshape(4, 8, mesh.shape["head"]), ("seq_0", "seq_1", "head"))
    placed = (
        P(None, SEQ, "head"),
        P(),
        P(None, "head"),
        P(None, "head"),
        P(None, "head"),
        P("head"),
        P(),
        P(None, "head"),
        P("head"),
        P(),
        P(None, "head"),
        P("head"),
        P("head"),
        P("head"),
        P("head"),
        P("head", None),
    )
    return jax.shard_map(
        body, mesh=torus, in_specs=placed, out_specs=P(None, SEQ, "head"), check_vma=False
    )
```

profile of v0, /device:TPU:1, one launch (start us, length us, event | category | flops | bytes accessed | tf_op | source)
XLA Modules:
  0.0 227.0 jit_solution(18370085318308386240)
XLA Ops:
  6.5 1.2 slice.141
  7.7 4.4 %collective-permute-start = (bf16[2,1,320]{1,2,0:T(8,128)(2,1)S(1)}, bf16[2,1,320]{1,2,0:T(8,128)(2,1)S(1)}, u32[]{:S(2)}, u32[]{:S(2)}) collective-permute-start(bf16[2,1,320]{1,2,0:T(8,128)(2,1)S(1)} %slice.141), channel_id=1, source_target_pairs={{0,8},{8,16},{16,24},{24,32},{32,40},{40,48},{48,56},{56,64},{64,7... | collective-permute-start | bytes 3848 | tf_op jit(solution)/shard_map/ppermute | solution.py:15
  12.1 0.9 copy_bitcast_fusion
  13.0 1.9 collective-permute-done
  14.9 2.0 copy.177
  17.0 0.8 copy.124
  18.1 32.8 %all-gather.11.cloned.1.call-done = bf16[8,320,258]{1,2,0:T(8,128)(2,1)} async-done(((bf16[1,320,258]{1,2,0:T(8,128)(2,1)}), bf16[8,320,258]{1,2,0:T(8,128)(2,1)}) %all-gather.11.cloned.1.call-update) | async-done | bytes 1320976 | tf_op jit(solution)/shard_map/all_gather | solution.py:22
  50.9 1.6 copy.125
  52.5 2.4 %reshape.160 = bf16[2560,258]{0,1:T(8,128)(2,1)} reshape(bf16[8,320,258]{1,0,2:T(8,128)(2,1)S(1)} %copy.125) | data formatting | bytes 2641920
  54.9 1.4 split.8
  56.3 0.8 slice_bitcast_fusion
  57.2 3.4 %fusion.3 = (bf16[2,128,2560]{2,1,0:T(8,128)(2,1)}, bf16[2,128,2560]{2,1,0:T(8,128)(2,1)S(1)}, bf16[2,128,2560]{2,1,0:T(8,128)(2,1)}, bf16[2,128,2560]{2,1,0:T(8,128)(2,1)}, bf16[2,128,2560]{2,1,0:T(8,128)(2,1)}) fusion(bf16[2,128,2560]{2,1,0:T(8,128)(2,1)S(1)} %bitcast.218, f32[2560]{0:T(1024)S(1)} %get-tuple-element.55, ...), kind=kLoop, calls=%fused_computation.12 | loop fusion | flops 13762560 | bytes 9226240 | tf_op jit(solution)/shard_map/convert_element_type | solution.py:114
  60.5 2.0 fusion.75
  62.9 1.3 copy.178
  64.2 1.3 copy.127
  65.5 2.3 %fusion.32 = f32[256,320]{0,1:T(8,128)S(1)} fusion(bf16[96,320]{1,0:T(8,128)(2,1)S(1)} %copy-done.39, bf16[256,2560]{1,0:T(8,128)(2,1)} %bitcast.226, bf16[2560,96]{0,1:T(8,128)(2,1)} %param.27, f32[320]{0:T(512)S(1)} %copy-done.41), kind=kOutput, calls=%fused_computation.66 | convolution fusion | flops 141910016 | bytes 2192640 | tf_op jit(solution)/shard_map/dot_general | solution.py:127
  67.9 1.2 reshape.129
  69.1 3.0 %fusion.134 = (f32[256,320]{0,1:T(8,128)S(1)}, f32[256,320]{0,1:T(8,128)}, f32[256,320]{0,1:T(8,128)}) fusion(f32[320]{0:T(512)S(1)} %copy-done.34, f32[320]{0:T(512)S(1)} %copy-done.35, f32[256,320]{0,1:T(8,128)} %copy-done.9, bf16[256,2560]{1,0:T(8,128)(2,1)S(1)} %bitcast.221, bf16[2560,320]{0,1:T(8,128)(2,1)} %param.21), kind=kOutput, calls=%fused_computation.205 | convolution fusion | flops 419921920 | bytes 4262400 | tf_op jit(solution)/shard_map/dot_general | solution.py:118
  72.1 1.4 reshape.127
  73.5 1.3 copy.133
  75.2 1.3 copy.147
  76.7 1.7 reduce_window_sum.11
  78.4 1.3 copy.134
  79.7 4.9 %bitcast_multiply_fusion = (bf16[2,5,2,64,64]{4,3,1,2,0:T(8,128)(2,1)}, bf16[2,5,2,64,64]{4,3,1,2,0:T(8,128)(2,1)S(1)}, bf16[2,5,2,64,64]{4,3,1,2,0:T(8,128)(2,1...) fusion(f32[2,2,64,5,64]{4,2,3,1,0:T(8,128)} %copy.147, ...), kind=kOutput, calls=%fused_computation.78 | convolution fusion | flops 421232640 | bytes 6077440 | tf_op jit(solution)/shard_map/dot_general | solution.py:118
  85.6 1.1 convolution_select_fusion.1
  88.2 3.1 %convolution_bitcast_fusion.2 = bf16[2,5,2,64,64]{4,3,1,2,0:T(8,128)(2,1)S(1)} fusion(bf16[2,2,64,2560,1]{3,2,4,1,0:T(8,128)(2,1)} %bitcast.224, bf16[5,64,2560,1,1]{2,1,0,4,3:T(8,128)(2,1)} %bitcast.235), kind=kOutput, calls=%fused_computation.39 | convolution fusion | flops 419430400 | bytes 3112960 | tf_op jit(solution)/shard_map/dot_general | solution.py:118
  91.6 1.5 fusion.17
  93.4 1.3 fusion.16
  94.6 1.1 fusion.13
  95.8 2.4 %while.12 = (s32[]{:T(128)}, f32[2,5,64,128]{3,2,1,0:T(8,128)S(1)}, f32[2,2,5,64,128]{4,3,2,1,0:T(8,128)}, bf16[2,2,5,64,64]{4,3,0,2,1:T(8,128)(2,1)}, f32[2,2,5,64,64]{4,3,0,2,1:T(8,128)S(1)}, /*index=5*/s32[]{:T(128)}) while((s32[]{:T(128)}, f32[2,5,64,128]{3,2,1,0:T(8,128)S(1)}, f32[2,2,5,64,128]{4,3,2,1,0:T(8,128)}, ...), condition=%wide.region_3.4_spmd, body=%wide.region_2.3_spmd.sunk | while | flops 10567682 | bytes 3441257 | solution.py:193
  95.8 0.8 bitcast_dynamic-update-slice_fusion.2
  97.0 0.8 bitcast_dynamic-update-slice_fusion.2
  98.2 0.7 copy-done.1
  99.2 38.7 %all-gather.7.cloned.1.call-done = f32[16,5,64,128]{3,2,1,0:T(8,128)} async-done(((f32[2,5,64,128]{3,2,1,0:T(8,128)}), f32[16,5,64,128]{3,2,1,0:T(8,128)}) %all-gather.7.cloned.1.call-update) | async-done | bytes 2621456 | tf_op jit(solution)/shard_map/all_gather | solution.py:41
  137.9 1.3 convolution_add_fusion.21
  139.2 0.7 copy-done.30
  139.8 1.3 convolution_add_fusion.20
  141.2 1.3 convolution_add_fusion.19
  142.5 0.7 copy-done.14
  143.2 1.3 convolution_add_fusion.18
  144.5 0.7 copy-done.16
  145.2 1.3 convolution_add_fusion.17
  146.5 0.7 copy-done.18
  147.2 1.3 convolution_add_fusion.16
  148.5 0.6 copy-done.20
  149.1 1.3 convolution_add_fusion.15
  150.5 0.7 copy-done.22
  151.1 2.0 convolution_add_fusion.14
  153.2 3.8 %copy.165 = bf16[320,2560]{0,1:T(8,128)(2,1)} copy(bf16[320,2560]{1,0:T(8,128)(2,1)} %param.33) | data formatting | bytes 3276800 | tf_op args[15]
  157.0 8.1 %all-to-all-start.1 = ((bf16[320,8,320]{0,2,1:T(8,128)(2,1)}), bf16[320,8,320]{0,2,1:T(8,128)(2,1)}, u32[]{:S(2)}, u32[]{:S(2)}) async-start(bf16[320,8,320]{0,2,1:T(8,128)(2,1)} %bitcast.220), calls=%async_computation.1 | async-start | bytes 3932160 | tf_op jit(solution)/shard_map/all_to_all | solution.py:208
  165.2 1.5 convolution_select_fusion.3
  166.7 1.2 fusion.144
  167.9 2.0 convolution_add_fusion.8
  170.3 11.1 %all-gather.9.cloned.1.call-done = f32[8,5,64,128]{3,2,1,0:T(8,128)} async-done(((f32[2,5,64,128]{3,2,1,0:T(8,128)}), f32[8,5,64,128]{3,2,1,0:T(8,128)}) %all-gather.9.cloned.1.call-update) | async-done | bytes 1310736 | tf_op jit(solution)/shard_map/all_gather | solution.py:41
  181.3 1.3 convolution_add_fusion.12
  182.6 1.3 convolution_add_fusion.11
  184.0 1.3 convolution_add_fusion.10
  185.3 2.2 fusion.28
  187.6 1.8 fusion.12
  189.4 1.2 fusion.45
  190.6 1.8 fusion.135
  194.1 23.6 %all_to_all.21 = bf16[8,256,320]{1,2,0:T(8,128)(2,1)S(1)} all-to-all(bf16[8,256,320]{1,2,0:T(8,128)(2,1)S(1)} %broadcast_in_dim.60), channel_id=1, replica_groups=mesh['seq_0'=4,'seq_1'=8,'head'=8] {'head'}, dimensions={0} | all-to-all | bytes 2621440 | tf_op jit(solution)/shard_map/all_to_all | solution.py:59
  217.7 2.1 fusion.39
  219.8 0.7 copy.248
  (136 shorter events, 7.5 us)
Async XLA Ops:
  6.5 73.2 %copy-start = (bf16[2560,320]{0,1:T(8,128)(2,1)S(1)}, bf16[2560,320]{0,1:T(8,128)(2,1)}, u32[]{:S(2)}) copy-start(bf16[2560,320]{0,1:T(8,128)(2,1)} %param.20) | copy-start | bytes 4915204
  6.5 11.5 %copy-start.33 = (f32[5,2560]{1,0:T(8,128)S(1)}, f32[5,2560]{1,0:T(8,128)}, u32[]{:S(2)}) copy-start(f32[5,2560]{1,0:T(8,128)} %param.19) | copy-start | bytes 153604
  6.5 44.4 %all-gather.11.cloned.1.call-start = ((), (), s32[]{:S(2)}) async-start(), calls=%async_computation.4 | async-start | bytes 1824768 | tf_op jit(solution)/shard_map/all_gather | solution.py:22
  7.7 7.2 %collective-permute-start = (bf16[2,1,320]{1,2,0:T(8,128)(2,1)S(1)}, bf16[2,1,320]{1,2,0:T(8,128)(2,1)S(1)}, u32[]{:S(2)}, u32[]{:S(2)}) collective-permute-start(bf16[2,1,320]{1,2,0:T(8,128)(2,1)S(1)} %slice.141), channel_id=1, source_target_pairs={{0,8},{8,16},{16,24},{24,32},{32,40},{40,48},{48,56},{56,64},{64,7... | collective-permute-start | bytes 3848 | tf_op jit(solution)/shard_map/ppermute | solution.py:15
  17.8 120.0 %all-gather.7.cloned.1.call-start = ((), (), s32[]{:S(2)}) async-start(), calls=%async_computation.2 | async-start | bytes 2949120 | tf_op jit(solution)/shard_map/all_gather | solution.py:41
  57.1 3.4 %copy-start.38 = (bf16[96,320]{1,0:T(8,128)(2,1)S(1)}, bf16[96,320]{1,0:T(8,128)(2,1)}, u32[]{:S(2)}) copy-start(bf16[96,320]{1,0:T(8,128)(2,1)} %param.25) | copy-start | bytes 184324
  57.1 3.4 %copy-start.40 = (f32[320]{0:T(512)S(1)}, f32[320]{0:T(512)}, u32[]{:S(2)}) copy-start(f32[320]{0:T(512)} %param.23) | copy-start | bytes 3844
  62.5 3.0 %copy-start.39 = (bf16[96,320]{1,0:T(8,128)(2,1)S(1)}, bf16[96,320]{1,0:T(8,128)(2,1)}, u32[]{:S(2)}) copy-start(bf16[96,320]{1,0:T(8,128)(2,1)} %param.28) | copy-start | bytes 184324
  62.5 3.0 %copy-start.41 = (f32[320]{0:T(512)S(1)}, f32[320]{0:T(512)}, u32[]{:S(2)}) copy-start(f32[320]{0:T(512)} %param.26) | copy-start | bytes 3844
  65.5 3.6 %copy-start.2 = (bf16[2,128,2560]{2,1,0:T(8,128)(2,1)S(1)}, bf16[2,128,2560]{2,1,0:T(8,128)(2,1)}, u32[]{:S(2)}) copy-start(bf16[2,128,2560]{2,1,0:T(8,128)(2,1)} %get-tuple-element.74) | copy-start | bytes 3932164
  65.5 3.6 %copy-start.34 = (f32[320]{0:T(512)S(1)}, f32[320]{0:T(512)}, u32[]{:S(2)}) copy-start(f32[320]{0:T(512)} %param.29) | copy-start | bytes 3844
  65.5 3.6 %copy-start.35 = (f32[320]{0:T(512)S(1)}, f32[320]{0:T(512)}, u32[]{:S(2)}) copy-start(f32[320]{0:T(512)} %param.30) | copy-start | bytes 3844
  67.9 1.2 copy-start.9
  72.1 2.7 %copy-start.8 = (f32[256,320]{0,1:T(8,128)S(1)}, f32[256,320]{0,1:T(8,128)}, u32[]{:S(2)}) copy-start(f32[256,320]{0,1:T(8,128)} %get-tuple-element.93) | copy-start | bytes 983044
  75.2 3.2 %copy-start.6 = (f32[2,2,64,5,64]{2,1,0,4,3:T(2,128)S(1)}, f32[2,2,64,5,64]{2,1,0,4,3:T(2,128)}, u32[]{:S(2)}) copy-start(f32[2,2,64,5,64]{2,1,0,4,3:T(2,128)} %reshape.129) | copy-start | bytes 983044
  78.3 6.2 %copy-start.3 = (f32[2,5,2,64,64]{4,3,2,1,0:T(8,128)}, f32[2,5,2,64,64]{4,3,2,1,0:T(8,128)S(1)}, u32[]{:S(2)}) copy-start(f32[2,5,2,64,64]{4,3,2,1,0:T(8,128)S(1)} %reduce_window_sum.11) | copy-start | bytes 983044
  84.6 0.8 copy-start.25
  84.6 1.0 copy-start.24
  88.2 3.1 %copy-start.28 = (bf16[2,5,2,64,64]{4,3,1,2,0:T(8,128)(2,1)S(1)}, bf16[2,5,2,64,64]{4,3,1,2,0:T(8,128)(2,1)}, u32[]{:S(2)}) copy-start(bf16[2,5,2,64,64]{4,3,1,2,0:T(8,128)(2,1)} %get-tuple-element.88) | copy-start | bytes 491524
  91.3 1.7 copy-start.26
  91.6 3.1 %copy-start.11 = (bf16[2,5,2,64,64]{4,3,2,1,0:T(8,128)(2,1)}, bf16[2,5,2,64,64]{4,3,2,1,0:T(8,128)(2,1)S(1)}, u32[]{:S(2)}) copy-start(bf16[2,5,2,64,64]{4,3,2,1,0:T(8,128)(2,1)S(1)} %fusion.51) | copy-start | bytes 491524
  93.1 1.6 copy-start.27
  95.8 42.1 %copy-start.32 = (pred[128]{0:T(512)(128)(4,1)S(1)}, pred[128]{0:T(512)(128)(4,1)}, u32[]{:S(2)}) copy-start(pred[128]{0:T(512)(128)(4,1)} %constant.67.clone.1) | copy-start | bytes 388
  95.8 1.0 copy-start.7
  97.0 1.0 copy-start.7
  98.2 0.7 copy-start.1
  98.9 82.4 %all-gather.9.cloned.1.call-start = ((), (), s32[]{:S(2)}) async-start(), calls=%async_computation.3 | async-start | bytes 1638400 | tf_op jit(solution)/shard_map/all_gather | solution.py:41
  139.2 0.7 copy-start.30
  142.5 0.7 copy-start.14
  144.5 0.7 copy-start.16
  146.5 0.7 copy-start.18
  148.5 0.7 copy-start.20
  150.5 0.7 copy-start.22
  157.0 37.0 %all-to-all-start.1 = ((bf16[320,8,320]{0,2,1:T(8,128)(2,1)}), bf16[320,8,320]{0,2,1:T(8,128)(2,1)}, u32[]{:S(2)}, u32[]{:S(2)}) async-start(bf16[320,8,320]{0,2,1:T(8,128)(2,1)} %bitcast.220), calls=%async_computation.1 | async-start | bytes 3932160 | tf_op jit(solution)/shard_map/all_to_all | solution.py:208
  165.1 2.8 %copy-start.4 = (f32[2,5,2,64,64]{4,3,2,1,0:T(8,128)S(1)}, f32[2,5,2,64,64]{4,3,2,1,0:T(8,128)}, u32[]{:S(2)}) copy-start(f32[2,5,2,64,64]{4,3,2,1,0:T(8,128)} %copy-done.3) | copy-start | bytes 983044
  165.1 2.8 %copy-start.13 = (f32[2,5,2,64,64]{4,3,1,2,0:T(8,128)S(1)}, f32[2,5,2,64,64]{4,3,1,2,0:T(8,128)}, u32[]{:S(2)}) copy-start(f32[2,5,2,64,64]{4,3,1,2,0:T(8,128)} %get-tuple-element.94) | copy-start | bytes 983044
  166.6 3.2 %copy-start.12 = (f32[2,5,64,128]{3,2,1,0:T(8,128)S(1)}, f32[2,5,64,128]{3,2,1,0:T(8,128)}, u32[]{:S(2)}) copy-start(f32[2,5,64,128]{3,2,1,0:T(8,128)} %convolution_add_fusion.14) | copy-start | bytes 983044
  166.7 3.2 %copy-start.15 = (bf16[2,5,64,128]{3,2,1,0:T(8,128)(2,1)S(1)}, bf16[2,5,64,128]{3,2,1,0:T(8,128)(2,1)}, u32[]{:S(2)}) copy-start(bf16[2,5,64,128]{3,2,1,0:T(8,128)(2,1)} %copy-done.14) | copy-start | bytes 491524
  166.7 3.2 %copy-start.17 = (bf16[2,5,64,128]{3,2,1,0:T(8,128)(2,1)S(1)}, bf16[2,5,64,128]{3,2,1,0:T(8,128)(2,1)}, u32[]{:S(2)}) copy-start(bf16[2,5,64,128]{3,2,1,0:T(8,128)(2,1)} %copy-done.16) | copy-start | bytes 491524
  166.7 3.2 %copy-start.19 = (bf16[2,5,64,128]{3,2,1,0:T(8,128)(2,1)S(1)}, bf16[2,5,64,128]{3,2,1,0:T(8,128)(2,1)}, u32[]{:S(2)}) copy-start(bf16[2,5,64,128]{3,2,1,0:T(8,128)(2,1)} %copy-done.18) | copy-start | bytes 491524
  166.7 3.2 %copy-start.21 = (bf16[2,5,64,128]{3,2,1,0:T(8,128)(2,1)S(1)}, bf16[2,5,64,128]{3,2,1,0:T(8,128)(2,1)}, u32[]{:S(2)}) copy-start(bf16[2,5,64,128]{3,2,1,0:T(8,128)(2,1)} %copy-done.20) | copy-start | bytes 491524
  166.7 3.2 %copy-start.23 = (bf16[2,5,64,128]{3,2,1,0:T(8,128)(2,1)S(1)}, bf16[2,5,64,128]{3,2,1,0:T(8,128)(2,1)}, u32[]{:S(2)}) copy-start(bf16[2,5,64,128]{3,2,1,0:T(8,128)(2,1)} %copy-done.22) | copy-start | bytes 491524
  166.7 3.2 %copy-start.31 = (bf16[2,5,64,128]{3,2,1,0:T(8,128)(2,1)S(1)}, bf16[2,5,64,128]{3,2,1,0:T(8,128)(2,1)}, u32[]{:S(2)}) copy-start(bf16[2,5,64,128]{3,2,1,0:T(8,128)(2,1)} %copy-done.30) | copy-start | bytes 491524
  170.2 15.1 %copy-start.29 = (f32[2,5,64,128]{3,2,1,0:T(8,128)}, f32[2,5,64,128]{3,2,1,0:T(8,128)S(1)}, u32[]{:S(2)}) copy-start(f32[2,5,64,128]{3,2,1,0:T(8,128)S(1)} %convolution_add_fusion.13) | copy-start | bytes 983044
  185.3 4.1 %copy-start.10 = (bf16[2,5,2,64,64]{4,3,1,2,0:T(8,128)(2,1)S(1)}, bf16[2,5,2,64,64]{4,3,1,2,0:T(8,128)(2,1)}, u32[]{:S(2)}) copy-start(bf16[2,5,2,64,64]{4,3,1,2,0:T(8,128)(2,1)} %convolution_add_fusion.8) | copy-start | bytes 491524
  187.6 3.1 %copy-start.5 = (f32[2,5,2,64,64]{3,4,2,1,0:T(8,128)S(1)}, f32[2,5,2,64,64]{3,4,2,1,0:T(8,128)}, u32[]{:S(2)}) copy-start(f32[2,5,2,64,64]{3,4,2,1,0:T(8,128)} %fusion.144) | copy-start | bytes 983044
  192.4 1.4 copy-start.36
  192.4 1.4 copy-start.37
Sparse Core Ops, SparseCore 0:
  17.9 32.9 all-gather.10
  99.0 38.7 all-gather.6
  153.3 27.9 all-gather.8
where the time goes:
time: 228 us; the launch traced here: 227 us
  waiting for transfers between devices  84.5 us (37%)
  matrix products  52.8 us (23%)
  local copies, waits for them, and re-layouts  34 us (15%)
  blocking collectives  23.6 us (10%)
  between operations  13.9 us (6%)
  starting transfers between devices  12.8 us (6%)
  other arithmetic  5.44 us (2%)
    all_gather x2, waiting for transfers between devices, prefix_by_axis(): pieces = lax.all_gather(running, axis)  49.7 us
    all_gather x1, waiting for transfers between devices, gather_turned(): out = lax.all_gather(both, axis, axis=0, tiled=True)  32.8 us
    dot_general x31, matrix products, matmul(): return jnp.matmul(left, right)  30 us
    all_to_all x1, blocking collectives, from_everyone(): return lax.all_to_all(copies, axis, split_axis=0, concat_axis=0, tiled=True)  23.6 us
    unnamed x84, local copies, waits for them, and re-layouts  11 us
    dot_general x3, matrix products, body(): jnp.dot(blended, weight_rows, preferred_element_type=jnp.float32)  10.9 us
    all_to_all x1, starting transfers between devices, body(): lax.all_to_all(output_weight, 'head', split_axis=1, concat_axis=0, tiled=...  8.09 us
    reshape x6, local copies, waits for them, and re-layouts, arrange(): values.reshape(seq_count, span_count, SPAN, head_count, HEAD_SIZE)  5.87 us
  transfers between devices with their start and end apart: 5, of which 4 were waited for; matrix products, arithmetic and copies ran while one was open for 10% of the time, Pallas kernels for 0%

commit v1 on v0

v1 whole, which is shorter than its diff:
```python
import functools
import jax
import jax.numpy as jnp
from jax import lax
from jax.experimental import pallas as pl
from jax.experimental.pallas import tpu as pltpu
from jax.sharding import Mesh
from jax.sharding import PartitionSpec as P

HEAD = 64
SPAN = 64
SEQ = ("seq_0", "seq_1")
BF = jnp.bfloat16
F32 = jnp.float32
WORK = 2
VM = pl.BlockSpec(memory_space=pltpu.VMEM)
SM = pl.BlockSpec(memory_space=pltpu.SMEM)


def mm(a, b, ca=1, cb=0):
    return lax.dot_general(a, b, (((ca,), (cb,)), ((), ())), preferred_element_type=F32)


def split3(a):
    hi = a.astype(BF)
    rest = a - hi.astype(F32)
    mid = rest.astype(BF)
    low = (rest - mid.astype(F32)).astype(BF)
    return hi, mid, low


def head_ones(width):
    i = lax.broadcasted_iota(jnp.int32, (width, width), 0) // HEAD
    j = lax.broadcasted_iota(jnp.int32, (width, width), 1) // HEAD
    return (i == j).astype(F32).astype(BF)


def head_sums(a):
    hi, mid, low = split3(a)
    ones = head_ones(a.shape[1])
    return mm(hi, ones) + mm(mid, ones) + mm(low, ones)


def local_kernel(seqs, length, width, *refs):
    (order, p0, p1, p2, p3, p4, p5, p6, p7, near, far, mix, wr, wk, wv, wd, wl, base_d, up_d, base_l, up_l,
     scale, blend, maps_ref, query_ref, local_ref, accr, acck, accv, accd, accl) = refs
    pieces = (p0, p1, p2, p3, p4, p5, p6, p7)
    rows = seqs * length
    heads = width // HEAD
    spans = length // SPAN
    accs = (accr, accd, acck, accv, accl)
    weights = (wr, wd, wk, wv, wl)
    at = lax.broadcasted_iota(jnp.int32, (rows, width), 0)
    for k, piece in enumerate(pieces):
        cur = piece[...].astype(F32).reshape(rows, width)
        edges = near if k < 4 else far
        prev = pltpu.roll(cur, 1, 0)
        for s in range(seqs):
            row = edges[k % 4, s : s + 1, :].astype(F32)
            prev = jnp.where(at == s * length, row, prev)
        change = prev - cur
        where = order[k]
        m = mix[where]
        start = pl.multiple_of(where * width, 64)
        for j in range(5):
            b = (cur + change * m[j : j + 1, :]).astype(BF)
            out = mm(b, weights[j][pl.ds(start, width), :])
            if k == 0:
                accs[j][...] = out
            else:
                accs[j][...] += out
    recept = accr[...]
    key_raw = acck[...]
    value = accv[...]
    hidden_d = jnp.tanh(accd[...]).astype(BF)
    hidden_l = accl[...].astype(BF)
    arg_d = base_d[...] + mm(hidden_d, up_d[...])
    decay = -(jax.nn.sigmoid(arg_d) * 0.6065306597126334)
    rate = jax.nn.sigmoid(base_l[...] + mm(hidden_l, up_l[...]))
    scaled = key_raw * scale[...]
    unit = scaled * lax.rsqrt(head_sums(scaled * scaled) + 1e-06)
    key = key_raw * (1.0 + (rate - 1.0) * blend[...])
    ri = lax.broadcasted_iota(jnp.int32, (rows, rows), 0)
    ci = lax.broadcasted_iota(jnp.int32, (rows, rows), 1)
    tri = ((ri // SPAN == ci // SPAN) & (ri >= ci)).astype(F32).astype(BF)
    d_hi, d_mid, d_low = split3(decay)
    cumul = mm(tri, d_hi) + mm(tri, d_mid) + mm(tri, d_low)
    groups = rows // SPAN
    c3 = cumul.reshape(groups, SPAN, width)
    middle = c3[:, SPAN // 2 - 1 : SPAN // 2, :]
    ending = c3[:, SPAN - 1 :, :]
    rel = (c3 - middle).reshape(rows, width)
    e_mid = jnp.exp(middle)
    e_end = jnp.exp(ending)
    e_tail = jnp.exp(ending - middle)
    grow = jnp.exp(rel)
    shrink = jnp.exp(-rel)

    def spread(small, a):
        return (a.reshape(groups, SPAN, width) * small).reshape(rows, width)

    l_alpha = -unit * jnp.exp(rel - decay)
    l_recept = recept * grow
    r_beta = unit * rate * shrink
    r_key = key * shrink
    beta_end = spread(e_tail, r_beta)
    key_end = spread(e_tail, r_key)
    alpha_dec = spread(e_mid, l_alpha)
    recept_dec = spread(e_mid, l_recept)
    la, lr, rb, rk, vb = (a.astype(BF) for a in (l_alpha, l_recept, r_beta, r_key, value))
    gi = lax.broadcasted_iota(jnp.int32, (2 * SPAN, 2 * SPAN), 0)
    gj = lax.broadcasted_iota(jnp.int32, (2 * SPAN, 2 * SPAN), 1)
    keep = (gi % SPAN > gj % SPAN) | ((gi >= SPAN) & (gi % SPAN == gj % SPAN))
    eye = lax.broadcasted_iota(jnp.int32, (HEAD, HEAD), 0) == lax.broadcasted_iota(jnp.int32, (HEAD, HEAD), 1)
    units = [(s, h, c) for s in range(seqs) for h in range(heads) for c in range(spans)]

    def cut(a, u):
        s, h, c = u
        r0 = s * length + c * SPAN
        return a[r0 : r0 + SPAN, h * HEAD : (h + 1) * HEAD]

    powers, sols, outs, values = [], [], [], []
    for u in units:
        left = jnp.concatenate([cut(la, u), cut(lr, u)], axis=0)
        right = jnp.concatenate([cut(rb, u), cut(rk, u)], axis=0)
        g = jnp.where(keep, mm(left, right, 1, 1), 0.0).astype(BF)
        v = cut(vb, u)
        powers.append(g[:SPAN, :SPAN])
        outs.append(g[SPAN:, :])
        values.append(v)
        sols.append(jnp.concatenate([cut(alpha_dec, u), mm(g[:SPAN, SPAN:], v)], axis=1))
    levels = SPAN.bit_length() - 1
    for level in range(levels):
        for i in range(len(units)):
            if level < levels - 1:
                both = jnp.concatenate([sols[i].astype(BF), powers[i]], axis=1)
                y = mm(powers[i], both)
                sols[i] = sols[i] + y[:, : 2 * HEAD]
                powers[i] = y[:, 2 * HEAD :].astype(BF)
            else:
                sols[i] = sols[i] + mm(powers[i], sols[i].astype(BF))
    moves = []
    for i, u in enumerate(units):
        s, h, c = u
        v = values[i]
        rhs = jnp.concatenate([sols[i].astype(BF), jnp.concatenate([jnp.zeros_like(v), v], axis=1)], axis=0)
        ends = jnp.concatenate([cut(beta_end, u), cut(key_end, u)], axis=0)
        lhs = jnp.concatenate([outs[i], jnp.transpose(ends).astype(BF)], axis=0)
        y = mm(lhs, rhs)
        query = cut(recept_dec, u) + y[:SPAN, :HEAD]
        local = y[:SPAN, HEAD:]
        last = e_end[s * spans + c, :, h * HEAD : (h + 1) * HEAD]
        trans = y[SPAN:, :HEAD] + jnp.where(eye, last, 0.0)
        moves.append((query, local, trans, y[SPAN:, HEAD:]))
    half = HEAD // WORK
    for p in range(seqs * heads):
        q0, l0, t0, n0 = moves[2 * p]
        q1, l1, t1, n1 = moves[2 * p + 1]
        first = jnp.concatenate([t0, n0], axis=1).astype(BF)
        y = mm(jnp.concatenate([q1, t1], axis=0).astype(BF), first)
        query_ref[p, 0:SPAN, :] = q0.astype(BF)
        query_ref[p, SPAN:, :] = y[:SPAN, :HEAD].astype(BF)
        local_ref[p, 0:SPAN, :] = l0
        local_ref[p, SPAN:, :] = y[:SPAN, HEAD:] + l1
        trans = y[SPAN:, :HEAD] - jnp.where(eye, 1.0, 0.0)
        incr = y[SPAN:, HEAD:] + n1
        packed = jnp.concatenate([trans[:32], trans[32:]], axis=1).astype(BF)
        for w in range(WORK):
            part = incr[:, w * half : (w + 1) * half]
            block = jnp.concatenate([part[16 * i : 16 * i + 16] for i in range(4)], axis=1).astype(BF)
            maps_ref[p * WORK + w, 0:32, :] = packed
            maps_ref[p * WORK + w, 32:48, :] = block
    for w in range(seqs * heads * WORK, maps_ref.shape[0]):
        maps_ref[w] = jnp.zeros(maps_ref.shape[1:], BF)


def prefix_kernel(maps_ref, states_ref):
    steps = maps_ref.shape[0]
    group = 8
    groups = steps // group
    half = HEAD // WORK
    eye = (
        lax.broadcasted_iota(jnp.int32, (HEAD, HEAD), 0) == lax.broadcasted_iota(jnp.int32, (HEAD, HEAD), 1)
    ).astype(F32)
    start = jnp.concatenate([eye, jnp.zeros((HEAD, half), F32)], axis=1)

    def load(i):
        packed = maps_ref[i, 0:32, :]
        trans = jnp.concatenate([packed[:, :HEAD], packed[:, HEAD:]], axis=0)
        block = maps_ref[i, 32:48, :]
        incr = jnp.concatenate([block[:, 32 * j : 32 * j + 32] for j in range(4)], axis=0).astype(F32)
        return trans, incr

    run = [start] * groups
    seen = {}
    for i in range(group):
        for g in range(groups):
            seen[g, i] = run[g]
            trans, incr = load(g * group + i)
            add = mm(trans, run[g].astype(BF))
            run[g] = run[g] + add + jnp.concatenate([jnp.zeros((HEAD, HEAD), F32), incr], axis=1)
    state = jnp.zeros((HEAD, half), F32)
    for g in range(groups):
        sb = state.astype(BF)
        for i in range(group):
            a = seen[g, i]
            if i == 0:
                here = state
            else:
                here = state + mm((a[:, :HEAD] - eye).astype(BF), sb) + a[:, HEAD:]
            states_ref[g * group + i] = jnp.concatenate([here[16 * j : 16 * j + 16] for j in range(4)], axis=1).astype(BF)
        state = state + mm((run[g][:, :HEAD] - eye).astype(BF), sb) + run[g][:, HEAD:]


def norm_kernel(seqs, length, width, core, states_ref, query_ref, local_ref, gain, bias, w_out, keep_ref, send_ref):
    heads = width // HEAD
    for s in range(seqs):
        cols = []
        for h in range(heads):
            p = s * heads + h
            halves = []
            for w in range(WORK):
                block = states_ref[p * WORK + w]
                halves.append(jnp.concatenate([block[:, 32 * j : 32 * j + 32] for j in range(4)], axis=0))
            state = jnp.concatenate(halves, axis=1)
            out = mm(query_ref[p], state) + local_ref[p]
            centred = out - jnp.mean(out, axis=1, keepdims=True)
            spread = jnp.mean(centred * centred, axis=1, keepdims=True)
            cols.append(centred * lax.rsqrt(spread + 0.00064))
        normed = (jnp.concatenate(cols, axis=1) * gain[...] + bias[...]).astype(BF)

        @pl.when(core[0] == s)
        def _():
            keep_ref[...] = normed

        @pl.when(core[0] != s)
        def _():
            send_ref[...] = mm(normed, w_out[...]).astype(BF)


def sum_kernel(width, where, keep_ref, got_ref, w_out, own_ref, *sends):
    wide = 2 * width
    x = where[0]
    for i, out in enumerate((own_ref,) + sends):
        block = lax.rem(x + i, 4)
        cols = pl.ds(pl.multiple_of(block * wide, 128), wide)
        total = mm(keep_ref[...], w_out[:, cols]) + got_ref[:, cols].astype(F32)
        out[...] = total.astype(out.dtype)


def fold_kernel(width, core, own_ref, a_ref, b_ref, c_ref, mine_ref, give_ref):
    total = own_ref[...] + a_ref[...].astype(F32) + b_ref[...].astype(F32) + c_ref[...].astype(F32)
    low, high = total[:, :width].astype(BF), total[:, width:].astype(BF)

    @pl.when(core[0] == 0)
    def _():
        mine_ref[...] = low
        give_ref[...] = high

    @pl.when(core[0] != 0)
    def _():
        mine_ref[...] = high
        give_ref[...] = low


def place_kernel(core, mine_ref, got_ref, out_ref):
    out_ref[core[0]] = mine_ref[...]
    out_ref[1 - core[0]] = got_ref[...]


def body(
    tokens,
    token_mix,
    receptance,
    key_weight,
    value_weight,
    decay_base,
    decay_down_matrix,
    decay_up_matrix,
    learn_base,
    learning_down_matrix,
    learning_up_matrix,
    key_scale,
    key_blend,
    norm_gain,
    norm_bias,
    output_weight,
):
    seqs, length, width = tokens.shape
    rows = seqs * length
    heads = width // HEAD
    n_head = lax.axis_size("head")
    n_seq = lax.axis_size("seq_0") * lax.axis_size("seq_1")
    me = lax.axis_index("head")
    core = lax.rem(me, 2)
    core_s = core.reshape(1).astype(jnp.int32)
    x_s = (me // 2).reshape(1).astype(jnp.int32)

    def turn(v, d):
        return lax.ppermute(v, "head", [(i, (i + d) % n_head) for i in range(n_head)])

    def swap(v):
        return lax.ppermute(v, "head", [(i, i ^ 1) for i in range(n_head)])

    near = [tokens] + [turn(tokens, d) for d in (2, 4, 6)]
    far = [swap(a) for a in near]
    last = jnp.stack([a[:, length - 1, :] for a in near])
    edge_near = lax.ppermute(last, SEQ, [(i, i + 1) for i in range(n_seq - 1)])
    edge_far = swap(edge_near)
    offsets = jnp.array([0, 6, 4, 2], jnp.int32)
    order = jnp.concatenate([lax.rem(me + offsets, n_head), lax.rem((me ^ 1) + offsets, n_head)]).astype(jnp.int32)
    mix = jnp.transpose(token_mix.reshape(5, n_head, width), (1, 0, 2))
    row = lambda a: a.reshape(1, width)
    pairs = seqs * heads
    low = decay_down_matrix.shape[1]
    maps, query, local = pl.pallas_call(
        functools.partial(local_kernel, seqs, length, width),
        out_shape=[
            jax.ShapeDtypeStruct((n_seq, 48, 128), BF),
            jax.ShapeDtypeStruct((pairs, length, HEAD), BF),
            jax.ShapeDtypeStruct((pairs, length, HEAD), F32),
        ],
        in_specs=[SM] + [VM] * 22,
        out_specs=[VM] * 3,
        scratch_shapes=[pltpu.VMEM((rows, width), F32)] * 3 + [pltpu.VMEM((rows, low), F32)] * 2,
        name="local",
    )(
        order, *near, *far, edge_near, edge_far, mix, receptance, key_weight, value_weight,
        decay_down_matrix, learning_down_matrix, row(decay_base), decay_up_matrix, row(learn_base),
        learning_up_matrix, row(key_scale), row(key_blend),
    )
    got = lax.all_to_all(maps, SEQ, split_axis=0, concat_axis=0, tiled=True)
    states = pl.pallas_call(
        prefix_kernel,
        out_shape=jax.ShapeDtypeStruct((n_seq, 16, 128), BF),
        in_specs=[VM],
        out_specs=VM,
        name="prefix",
    )(got)
    states = lax.all_to_all(states, SEQ, split_axis=0, concat_axis=0, tiled=True)
    full = output_weight.shape[1]
    keep, send = pl.pallas_call(
        functools.partial(norm_kernel, seqs, length, width),
        out_shape=[jax.ShapeDtypeStruct((length, width), BF), jax.ShapeDtypeStruct((length, full), BF)],
        in_specs=[SM] + [VM] * 6,
        out_specs=[VM] * 2,
        name="norm",
    )(core_s, states, query, local, row(norm_gain), row(norm_bias), output_weight)
    half = swap(send)
    wide = 2 * width
    own, s1, s2, s3 = pl.pallas_call(
        functools.partial(sum_kernel, width),
        out_shape=[jax.ShapeDtypeStruct((length, wide), F32)] + [jax.ShapeDtypeStruct((length, wide), BF)] * 3,
        in_specs=[SM] + [VM] * 3,
        out_specs=[VM] * 4,
        name="partial",
    )(x_s, keep, half, output_weight)
    parts = [turn(s1, 2), turn(s2, 4), turn(s3, 6)]
    mine, give = pl.pallas_call(
        functools.partial(fold_kernel, width),
        out_shape=[jax.ShapeDtypeStruct((length, width), BF)] * 2,
        in_specs=[SM] + [VM] * 4,
        out_specs=[VM] * 2,
        name="fold",
    )(core_s, own, *parts)
    other = swap(give)
    return pl.pallas_call(
        place_kernel,
        out_shape=jax.ShapeDtypeStruct((seqs, length, width), BF),
        in_specs=[SM] + [VM] * 2,
        out_specs=VM,
        name="place",
    )(core_s, mine, other)


def solution(mesh):
    torus = Mesh(mesh.devices.reshape(4, 8, mesh.shape["head"]), ("seq_0", "seq_1", "head"))
    placed = (
        P(None, SEQ, "head"),
        P(),
        P(None, "head"),
        P(None, "head"),
        P(None, "head"),
        P("head"),
        P(),
        P(None, "head"),
        P("head"),
        P(),
        P(None, "head"),
        P("head"),
        P("head"),
        P("head"),
        P("head"),
        P("head", None),
    )
    return jax.shard_map(
        body, mesh=torus, in_specs=placed, out_specs=P(None, SEQ, "head"), check_vma=False
    )
```

time: 228 us -> 143 us (0.63)
  waiting for transfers between devices: 84.5 us -> 26.3 us
  matrix products: 52.8 us -> 0 us
  Pallas kernels: 0 us -> 30.4 us
  between operations: 13.9 us -> 0.14 us
  starting transfers between devices: 12.8 us -> 25.3 us
  other arithmetic: 5.44 us -> 1.33 us
    all_gather x3 -> x0, waiting for transfers between devices: 82.5 us -> none  [the longest x2 49.7 us: prefix_by_axis(): pieces = lax.all_gather(running, axis)]
    dot_general x43 -> x0, matrix products: 52.8 us -> none  [the longest x31 30 us: matmul(): return jnp.matmul(left, right)]
    pallas_call x0 -> x6, Pallas kernels: none -> 30.4 us  [the longest x1 15.6 us: body(): pl.pallas_call(functools.partial(local_kernel, seqs, length, width), out_...]
    ppermute x1 -> x14, waiting for transfers between devices: 1.92 us -> 18.6 us  [the longest x6 15.5 us: turn(): lax.ppermute(v, 'head', [(i, (i + d) % n_head) for i in range(n_head)])]
    ppermute x1 -> x14, starting transfers between devices: 4.37 us -> 17.7 us  [the longest x6 7.18 us: turn(): lax.ppermute(v, 'head', [(i, (i + d) % n_head) for i in range(n_head)])]
    ppermute x0 -> x6, local copies, waits for them, and re-layouts: none -> 9.78 us  [the longest x3 4.89 us: swap(): return lax.ppermute(v, 'head', [(i, i ^ 1) for i in range(n_head)])]
    reshape x12 -> x8, local copies, waits for them, and re-layouts: 12.7 us -> 4.21 us  [the longest x6 3.48 us: body(): row = lambda a: a.reshape(1, width)]
    all_to_all x1, waiting for transfers between devices: 0.01 us -> 7.74 us  [body(): lax.all_to_all(states, SEQ, split_axis=0, concat_axis=0, tiled=True)]
  transfers between devices with their start and end apart: 5 -> 15, of which waited for: 4 -> 9; matrix products, arithmetic and copies ran while one was open for 10% -> 21% of each run, Pallas kernels for 0% -> 0%
where the time goes in v1:
time: 143 us
  local copies, waits for them, and re-layouts  34.4 us (24%)
  Pallas kernels  30.4 us (21%)
  waiting for transfers between devices  26.3 us (18%)
  starting transfers between devices  25.3 us (18%)
  blocking collectives  24.8 us (17%)
    all_to_all x1, blocking collectives, body(): got = lax.all_to_all(maps, SEQ, split_axis=0, concat_axis=0, tiled=True)  24.8 us
    unnamed x47, local copies, waits for them, and re-layouts  16.7 us
    pallas_call x1, Pallas kernels, body(): pl.pallas_call(functools.partial(local_kernel, seqs, length, width), out_...  15.6 us
    ppermute x6, waiting for transfers between devices, turn(): lax.ppermute(v, 'head', [(i, (i + d) % n_head) for i in range(n_head)])  15.5 us
    all_to_all x1, waiting for transfers between devices, body(): lax.all_to_all(states, SEQ, split_axis=0, concat_axis=0, tiled=True)  7.74 us
    all_to_all x1, starting transfers between devices, body(): lax.all_to_all(states, SEQ, split_axis=0, concat_axis=0, tiled=True)  7.6 us
    ppermute x6, starting transfers between devices, turn(): lax.ppermute(v, 'head', [(i, (i + d) % n_head) for i in range(n_head)])  7.18 us
    ppermute x7, starting transfers between devices, swap(): return lax.ppermute(v, 'head', [(i, i ^ 1) for i in range(n_head)])  6.97 us
  transfers between devices with their start and end apart: 15, of which 9 were waited for; matrix products, arithmetic and copies ran while one was open for 21% of the time, Pallas kernels for 0%

profile of v1, /device:TPU:1, one launch (start us, length us, event | category | flops | bytes accessed | tf_op | source)
XLA Modules:
  0.0 142.6 jit_solution(15617442942961721146)
XLA Ops:
  0.0 1.1 copy.36
  1.1 3.4 %collective-permute-start.2 = (bf16[2,128,320]{2,0,1:T(2,128)(2,1)S(1)}, bf16[2,128,320]{2,0,1:T(2,128)(2,1)}, u32[]{:S(2)}, u32[]{:S(2)}) collective-permute-start(bf16[2,128,320]{2,0,1:T(2,128)(2,1)S(1)} %copy.36), channel_id=1, source_target_pairs={{0,6},{1,7},{2,0},{3,1},{4,2},{5,3},{6,4},{7,5},{8,14},{9,15},{10,... | collective-permute-start | bytes 491528 | tf_op jit(solution)/shard_map/ppermute | solution.py:300
  4.5 0.5 collective-permute-start.1
  5.0 0.6 collective-permute-start
  5.6 1.1 copy.42.refs_1_
  6.7 1.6 %collective-permute-start.3 = (bf16[2,128,320]{2,1,0:T(8,128)(2,1)S(1)}, bf16[2,128,320]{2,1,0:T(8,128)(2,1)}, u32[]{:S(2)}, u32[]{:S(2)}) collective-permute-start(bf16[2,128,320]{2,1,0:T(8,128)(2,1)S(1)} %copy.42.refs_1_), channel_id=1, source_target_pairs={{0,1},{1,0},{2,3},{3,2},{4,5},{5,4},{6,7},{7,6},{8,9},{9,8},{10,11... | collective-permute-start | bytes 491528 | tf_op jit(solution)/shard_map/ppermute | solution.py:303
  8.3 1.9 %collective-permute-done.2 = bf16[2,128,320]{2,0,1:T(2,128)(2,1)} collective-permute-done((bf16[2,128,320]{2,0,1:T(2,128)(2,1)S(1)}, bf16[2,128,320]{2,0,1:T(2,128)(2,1)}, u32[]{:S(2)}, u32[]{:S(2)}) %collective-permute-start.2) | collective-permute-done | bytes 163872 | tf_op jit(solution)/shard_map/ppermute | solution.py:300
  10.2 0.7 slice_bitcast_fusion
  10.9 0.7 collective-permute-done.1
  11.6 0.7 slice_bitcast_fusion.1
  12.3 4.8 %collective-permute-done = bf16[2,128,320]{2,0,1:T(2,128)(2,1)} collective-permute-done((bf16[2,128,320]{2,0,1:T(2,128)(2,1)S(1)}, bf16[2,128,320]{2,0,1:T(2,128)(2,1)}, u32[]{:S(2)}, u32[]{:S(2)}) %collective-permute-start) | collective-permute-done | bytes 163872 | tf_op jit(solution)/shard_map/ppermute | solution.py:300
  17.1 0.7 slice_bitcast_fusion.2
  17.8 3.5 %collective-permute-start.7 = (bf16[4,2,320]{2,1,0:T(2,128)(2,1)S(1)}, bf16[4,2,320]{2,1,0:T(2,128)(2,1)S(1)}, u32[]{:S(2)}, u32[]{:S(2)}) collective-permute-start(bf16[4,2,320]{2,1,0:T(2,128)(2,1)S(1)} %pad_maximum_fusion), channel_id=1, source_target_pairs={{0,8},{8,16},{16,24},{24,32},{32,40},{40,48},{48,56},{56,64},{64,7... | collective-permute-start | bytes 15368 | tf_op jit(solution)/shard_map/ppermute | solution.py:308
  21.4 0.9 collective-permute-start.4
  22.2 0.1 collective-permute-start.5
  22.3 0.4 collective-permute-start.6
  22.7 0.7 compare_select_fusion.2
  23.4 0.4 collective-permute-start.8
  23.8 0.7 pad_add_fusion.refs_0_
  24.4 3.9 %copy.49.refs_12_ = bf16[2560,320]{1,0:T(8,128)(2,1)} copy(bf16[2560,320]{0,1:T(8,128)(2,1)} %param.19) | data formatting | bytes 3276800 | tf_op args[2]
  28.4 0.0 copy-start.1
  28.4 2.4 %copy.50.refs_13_ = bf16[2560,320]{1,0:T(8,128)(2,1)} copy(bf16[2560,320]{0,1:T(8,128)(2,1)S(1)} %copy-done) | data formatting | bytes 3276800 | tf_op args[3]
  30.8 2.4 %copy.51.refs_14_ = bf16[2560,320]{1,0:T(8,128)(2,1)} copy(bf16[2560,320]{0,1:T(8,128)(2,1)S(1)} %copy-done.1) | data formatting | bytes 3276800 | tf_op args[4]
  33.3 0.0 copy-start.16
  33.3 1.1 copy.52.refs_15_
  34.4 1.1 copy.53.refs_16_
  35.5 0.1 reshape.29
  35.6 0.7 copy.56
  36.3 0.6 reshape.30.refs_17_
  36.9 0.5 reshape.31.refs_19_
  37.4 0.6 reshape.32.refs_21_
  38.0 0.6 reshape.33.refs_22_
  38.6 1.6 %copy.43.refs_2_ = bf16[2,128,320]{2,1,0:T(8,128)(2,1)} copy(bf16[2,128,320]{2,0,1:T(2,128)(2,1)} %collective-permute-done) | data formatting | bytes 327680 | tf_op jit(solution)/shard_map/ppermute | solution.py:300
  40.2 1.6 %copy.44.refs_3_ = bf16[2,128,320]{2,1,0:T(8,128)(2,1)} copy(bf16[2,128,320]{2,0,1:T(2,128)(2,1)} %collective-permute-done.1) | data formatting | bytes 327680 | tf_op jit(solution)/shard_map/ppermute | solution.py:300
  41.8 1.6 %copy.45.refs_4_ = bf16[2,128,320]{2,1,0:T(8,128)(2,1)} copy(bf16[2,128,320]{2,0,1:T(2,128)(2,1)} %collective-permute-done.2) | data formatting | bytes 327680 | tf_op jit(solution)/shard_map/ppermute | solution.py:300
  43.5 1.6 %copy.46.refs_6_ = bf16[2,128,320]{2,1,0:T(8,128)(2,1)} copy(bf16[2,128,320]{2,0,1:T(2,128)(2,1)} %collective-permute-done.4) | data formatting | bytes 327680 | tf_op jit(solution)/shard_map/ppermute | solution.py:303
  45.1 1.6 %copy.47.refs_7_ = bf16[2,128,320]{2,1,0:T(8,128)(2,1)} copy(bf16[2,128,320]{2,0,1:T(2,128)(2,1)} %collective-permute-done.5) | data formatting | bytes 327680 | tf_op jit(solution)/shard_map/ppermute | solution.py:303
  46.7 1.6 %copy.48.refs_8_ = bf16[2,128,320]{2,1,0:T(8,128)(2,1)} copy(bf16[2,128,320]{2,0,1:T(2,128)(2,1)} %collective-permute-done.6) | data formatting | bytes 327680 | tf_op jit(solution)/shard_map/ppermute | solution.py:303
  48.4 0.6 copy-done.13
  49.0 15.6 %local.1 = (bf16[32,48,128]{2,1,0:T(8,128)(2,1)}, bf16[10,128,64]{2,1,0:T(8,128)(2,1)}, f32[10,128,64]{2,1,0:T(8,128)}) custom-call(s32[8]{0:T(128)} %pad_add_fusion.refs_0_, bf16[2,128,320]{2,1,0:T(8,128)(2,1)} %copy-done.2, bf16[2,128,320]{2,1,0:T(8,128)(2,1)} %copy.43.refs_2_, bf16[2,128,320]{2,1,0:T(8,128)(2,1)} %copy.44.refs_3_, ...), custom_call_target="tpu_custom_call" | custom-call | tf_op jit(solution)/shard_map/local/pallas_call | solution.py:316
  64.6 24.8 %all_to_all.10.maps_ref = bf16[32,48,128]{2,1,0:T(8,128)(2,1)} all-to-all(bf16[32,48,128]{2,1,0:T(8,128)(2,1)} %get-tuple-element.16), channel_id=1, replica_groups=mesh['seq_0'=4,'seq_1'=8,'head'=8] {'seq_0','seq_1'}, dimensions={0} | all-to-all | bytes 786432 | tf_op jit(solution)/shard_map/all_to_all | solution.py:332
  89.4 3.7 %prefix.1 = bf16[32,16,128]{2,1,0:T(8,128)(2,1)} custom-call(bf16[32,48,128]{2,1,0:T(8,128)(2,1)} %all_to_all.10.maps_ref), custom_call_target="tpu_custom_call" | custom-call | tf_op jit(solution)/shard_map/prefix/pallas_call | solution.py:333
  93.0 7.6 %all-to-all-start.1 = ((bf16[32,16,128]{2,1,0:T(8,128)(2,1)}), bf16[32,16,128]{2,1,0:T(8,128)(2,1)S(1)}, u32[]{:S(2)}, u32[]{:S(2)}) async-start(bf16[32,16,128]{2,1,0:T(8,128)(2,1)} %prefix.1), calls=%async_computation.1 | async-start | bytes 262144 | tf_op jit(solution)/shard_map/all_to_all | solution.py:340
  100.7 0.6 reshape.34.gain
  101.2 0.6 reshape.35.bias
  101.8 7.7 %all-to-all-done.1.states_ref = bf16[32,16,128]{2,1,0:T(8,128)(2,1)S(1)} async-done(((bf16[32,16,128]{2,1,0:T(8,128)(2,1)}), bf16[32,16,128]{2,1,0:T(8,128)(2,1)S(1)}, u32[]{:S(2)}, u32[]{:S(2)}) %all-to-all-start.1) | async-done | bytes 131104 | tf_op jit(solution)/shard_map/all_to_all | solution.py:340
  109.6 0.7 copy-done.4
  110.2 4.5 %norm.1 = (bf16[128,320]{1,0:T(8,128)(2,1)}, bf16[128,2560]{1,0:T(8,128)(2,1)}) custom-call(s32[1]{0:T(128)} %bitcast.core, bf16[32,16,128]{2,1,0:T(8,128)(2,1)} %copy-done.4, bf16[10,128,64]{2,1,0:T(8,128)(2,1)} %get-tuple-element.17.query_ref, f32[10,128,64]{2,1,0:T(8,128)} %get-tuple-element.18.local_ref, f32[1,320]{1,0:T(1,128)} %reshape.34.gain, ...), custom_call_target="tpu_custom_call" | custom-call | tf_op jit(solution)/shard_map/norm/pallas_call | solution.py:342
  114.7 2.2 %collective-permute-start.9 = (bf16[128,2560]{1,0:T(8,128)(2,1)}, bf16[128,2560]{1,0:T(8,128)(2,1)S(1)}, u32[]{:S(2)}, u32[]{:S(2)}) collective-permute-start(bf16[128,2560]{1,0:T(8,128)(2,1)} %get-tuple-element.20), channel_id=1, source_target_pairs={{0,1},{1,0},{2,3},{3,2},{4,5},{5,4},{6,7},{7,6},{8,9},{9,8},{10,11... | collective-permute-start | bytes 1966088 | tf_op jit(solution)/shard_map/ppermute | solution.py:303
  116.9 1.9 %collective-permute-done.9.got_ref = bf16[128,2560]{1,0:T(8,128)(2,1)S(1)} collective-permute-done((bf16[128,2560]{1,0:T(8,128)(2,1)}, bf16[128,2560]{1,0:T(8,128)(2,1)S(1)}, u32[]{:S(2)}, u32[]{:S(2)}) %collective-permute-start.9) | collective-permute-done | bytes 655392 | tf_op jit(solution)/shard_map/ppermute | solution.py:303
  118.8 0.9 copy-done.3
  119.7 2.9 %partial.1 = (f32[128,640]{1,0:T(8,128)}, bf16[128,640]{1,0:T(8,128)(2,1)}, bf16[128,640]{1,0:T(8,128)(2,1)}, bf16[128,640]{1,0:T(8,128)(2,1)}) custom-call(s32[1]{0:T(128)} %bitcast.1.where, bf16[128,320]{1,0:T(8,128)(2,1)} %get-tuple-element.19.keep_ref, bf16[128,2560]{1,0:T(8,128)(2,1)} %copy-done.3, bf16[320,2560]{1,0:T(8,128)(2,1)} %w_out.3), custom_call_target="tpu_custom_call" | custom-call | tf_op jit(solution)/shard_map/partial/pallas_call | solution.py:351
  122.6 2.3 %collective-permute-start.11 = (bf16[128,640]{1,0:T(8,128)(2,1)}, bf16[128,640]{1,0:T(8,128)(2,1)S(1)}, u32[]{:S(2)}, u32[]{:S(2)}) collective-permute-start(bf16[128,640]{1,0:T(8,128)(2,1)} %get-tuple-element.23), channel_id=1, source_target_pairs={{0,4},{1,5},{2,6},{3,7},{4,0},{5,1},{6,2},{7,3},{8,12},{9,13},{10,... | collective-permute-start | bytes 491528 | tf_op jit(solution)/shard_map/ppermute | solution.py:300
  124.9 0.4 collective-permute-start.12
  125.3 4.5 %collective-permute-done.10.a_ref = bf16[128,640]{1,0:T(8,128)(2,1)S(1)} collective-permute-done((bf16[128,640]{1,0:T(8,128)(2,1)}, bf16[128,640]{1,0:T(8,128)(2,1)S(1)}, u32[]{:S(2)}, u32[]{:S(2)}) %collective-permute-start.10) | collective-permute-done | bytes 163872 | tf_op jit(solution)/shard_map/ppermute | solution.py:300
  129.8 2.8 %collective-permute-done.11.b_ref = bf16[128,640]{1,0:T(8,128)(2,1)S(1)} collective-permute-done((bf16[128,640]{1,0:T(8,128)(2,1)}, bf16[128,640]{1,0:T(8,128)(2,1)S(1)}, u32[]{:S(2)}, u32[]{:S(2)}) %collective-permute-start.11) | collective-permute-done | bytes 163872 | tf_op jit(solution)/shard_map/ppermute | solution.py:300
  132.6 0.7 collective-permute-done.12.c_ref
  133.3 0.7 copy-done.9
  134.0 2.1 %fold.1 = (bf16[128,320]{1,0:T(8,128)(2,1)}, bf16[128,320]{1,0:T(8,128)(2,1)}) custom-call(s32[1]{0:T(128)} %bitcast.core, f32[128,640]{1,0:T(8,128)} %get-tuple-element.21.own_ref, bf16[128,640]{1,0:T(8,128)(2,1)} %copy-done.7, bf16[128,640]{1,0:T(8,128)(2,1)} %copy-done.8, bf16[128,640]{1,0:T(8,128)(2,1)} %copy-done.9), custom_call_target="tpu_custom_call" | custom-call | tf_op jit(solution)/shard_map/fold/pallas_call | solution.py:359
  136.0 1.5 %collective-permute-start.13 = (bf16[128,320]{1,0:T(8,128)(2,1)}, bf16[128,320]{1,0:T(8,128)(2,1)S(1)}, u32[]{:S(2)}, u32[]{:S(2)}) collective-permute-start(bf16[128,320]{1,0:T(8,128)(2,1)} %get-tuple-element.26), channel_id=1, source_target_pairs={{0,1},{1,0},{2,3},{3,2},{4,5},{5,4},{6,7},{7,6},{8,9},{9,8},{10,11... | collective-permute-start | bytes 245768 | tf_op jit(solution)/shard_map/ppermute | solution.py:303
  137.5 1.2 collective-permute-done.13.got_ref
  138.6 0.6 copy-done.10
  139.3 1.6 %place.1 = bf16[2,128,320]{2,1,0:T(8,128)(2,1)} custom-call(s32[1]{0:T(128)} %bitcast.core, bf16[128,320]{1,0:T(8,128)(2,1)} %get-tuple-element.25.mine_ref, bf16[128,320]{1,0:T(8,128)(2,1)} %copy-done.10), custom_call_target="tpu_custom_call" | custom-call | tf_op jit(solution)/shard_map/place/pallas_call | solution.py:367
  140.9 1.7 %copy.54 = bf16[2,128,320]{1,2,0:T(8,128)(2,1)} copy(bf16[2,128,320]{2,1,0:T(8,128)(2,1)} %place.1) | data formatting | bytes 327680 | tf_op jit(solution)/shard_map/place/pallas_call | solution.py:367
  (42 shorter events, 0.1 us)
Async XLA Ops:
  1.1 9.1 %collective-permute-start.2 = (bf16[2,128,320]{2,0,1:T(2,128)(2,1)S(1)}, bf16[2,128,320]{2,0,1:T(2,128)(2,1)}, u32[]{:S(2)}, u32[]{:S(2)}) collective-permute-start(bf16[2,128,320]{2,0,1:T(2,128)(2,1)S(1)} %copy.36), channel_id=1, source_target_pairs={{0,6},{1,7},{2,0},{3,1},{4,2},{5,3},{6,4},{7,5},{8,14},{9,15},{10,... | collective-permute-start | bytes 491528 | tf_op jit(solution)/shard_map/ppermute | solution.py:300
  4.5 7.2 %collective-permute-start.1 = (bf16[2,128,320]{2,0,1:T(2,128)(2,1)S(1)}, bf16[2,128,320]{2,0,1:T(2,128)(2,1)}, u32[]{:S(2)}, u32[]{:S(2)}) collective-permute-start(bf16[2,128,320]{2,0,1:T(2,128)(2,1)S(1)} %copy.36), channel_id=1, source_target_pairs={{0,4},{1,5},{2,6},{3,7},{4,0},{5,1},{6,2},{7,3},{8,12},{9,13},{10,... | collective-permute-start | bytes 491528 | tf_op jit(solution)/shard_map/ppermute | solution.py:300
  5.0 12.1 %collective-permute-start = (bf16[2,128,320]{2,0,1:T(2,128)(2,1)S(1)}, bf16[2,128,320]{2,0,1:T(2,128)(2,1)}, u32[]{:S(2)}, u32[]{:S(2)}) collective-permute-start(bf16[2,128,320]{2,0,1:T(2,128)(2,1)S(1)} %copy.36), channel_id=1, source_target_pairs={{0,2},{1,3},{2,4},{3,5},{4,6},{5,7},{6,0},{7,1},{8,10},{9,11},{10,... | collective-permute-start | bytes 491528 | tf_op jit(solution)/shard_map/ppermute | solution.py:300
  6.7 21.7 %copy-start.2 = (bf16[2,128,320]{2,1,0:T(8,128)(2,1)}, bf16[2,128,320]{2,1,0:T(8,128)(2,1)S(1)}, u32[]{:S(2)}) copy-start(bf16[2,128,320]{2,1,0:T(8,128)(2,1)S(1)} %copy.42.refs_1_) | copy-start | bytes 491524
  6.7 41.7 %collective-permute-start.3 = (bf16[2,128,320]{2,1,0:T(8,128)(2,1)S(1)}, bf16[2,128,320]{2,1,0:T(8,128)(2,1)}, u32[]{:S(2)}, u32[]{:S(2)}) collective-permute-start(bf16[2,128,320]{2,1,0:T(8,128)(2,1)S(1)} %copy.42.refs_1_), channel_id=1, source_target_pairs={{0,1},{1,0},{2,3},{3,2},{4,5},{5,4},{6,7},{7,6},{8,9},{9,8},{10,11... | collective-permute-start | bytes 491528 | tf_op jit(solution)/shard_map/ppermute | solution.py:303
  17.8 5.6 %collective-permute-start.7 = (bf16[4,2,320]{2,1,0:T(2,128)(2,1)S(1)}, bf16[4,2,320]{2,1,0:T(2,128)(2,1)S(1)}, u32[]{:S(2)}, u32[]{:S(2)}) collective-permute-start(bf16[4,2,320]{2,1,0:T(2,128)(2,1)S(1)} %pad_maximum_fusion), channel_id=1, source_target_pairs={{0,8},{8,16},{16,24},{24,32},{32,40},{40,48},{48,56},{56,64},{64,7... | collective-permute-start | bytes 15368 | tf_op jit(solution)/shard_map/ppermute | solution.py:308
  21.4 22.1 %collective-permute-start.4 = (bf16[2,128,320]{2,0,1:T(2,128)(2,1)}, bf16[2,128,320]{2,0,1:T(2,128)(2,1)}, u32[]{:S(2)}, u32[]{:S(2)}) collective-permute-start(bf16[2,128,320]{2,0,1:T(2,128)(2,1)} %collective-permute-done), channel_id=1, source_target_pairs={{0,1},{1,0},{2,3},{3,2},{4,5},{5,4},{6,7},{7,6},{8,9},{9,8},{10,11... | collective-permute-start | bytes 491528 | tf_op jit(solution)/shard_map/ppermute | solution.py:303
  22.2 22.9 %collective-permute-start.5 = (bf16[2,128,320]{2,0,1:T(2,128)(2,1)}, bf16[2,128,320]{2,0,1:T(2,128)(2,1)}, u32[]{:S(2)}, u32[]{:S(2)}) collective-permute-start(bf16[2,128,320]{2,0,1:T(2,128)(2,1)} %collective-permute-done.1), channel_id=1, source_target_pairs={{0,1},{1,0},{2,3},{3,2},{4,5},{5,4},{6,7},{7,6},{8,9},{9,8},{10,11... | collective-permute-start | bytes 491528 | tf_op jit(solution)/shard_map/ppermute | solution.py:303
  22.3 24.4 %collective-permute-start.6 = (bf16[2,128,320]{2,0,1:T(2,128)(2,1)}, bf16[2,128,320]{2,0,1:T(2,128)(2,1)}, u32[]{:S(2)}, u32[]{:S(2)}) collective-permute-start(bf16[2,128,320]{2,0,1:T(2,128)(2,1)} %collective-permute-done.2), channel_id=1, source_target_pairs={{0,1},{1,0},{2,3},{3,2},{4,5},{5,4},{6,7},{7,6},{8,9},{9,8},{10,11... | collective-permute-start | bytes 491528 | tf_op jit(solution)/shard_map/ppermute | solution.py:303
  23.4 5.0 %copy-start.12 = (bf16[4,2,320]{2,1,0:T(2,128)(2,1)}, bf16[4,2,320]{2,1,0:T(2,128)(2,1)S(1)}, u32[]{:S(2)}) copy-start(bf16[4,2,320]{2,1,0:T(2,128)(2,1)S(1)} %collective-permute-done.7.refs_9_) | copy-start | bytes 15364
  23.4 25.0 %collective-permute-start.8 = (bf16[4,2,320]{2,1,0:T(2,128)(2,1)S(1)}, bf16[4,2,320]{2,1,0:T(2,128)(2,1)S(1)}, u32[]{:S(2)}, u32[]{:S(2)}) collective-permute-start(bf16[4,2,320]{2,1,0:T(2,128)(2,1)S(1)} %collective-permute-done.7.refs_9_), channel_id=1, source_target_pairs={{0,1},{1,0},{2,3},{3,2},{4,5},{5,4},{6,7},{7,6},{8,9},{9,8},{10,11... | collective-permute-start | bytes 15368 | tf_op jit(solution)/shard_map/ppermute | solution.py:303
  24.4 4.0 %copy-start = (bf16[2560,320]{0,1:T(8,128)(2,1)S(1)}, bf16[2560,320]{0,1:T(8,128)(2,1)}, u32[]{:S(2)}) copy-start(bf16[2560,320]{0,1:T(8,128)(2,1)} %param.20) | copy-start | bytes 4915204
  28.4 2.5 %copy-start.1 = (bf16[2560,320]{0,1:T(8,128)(2,1)S(1)}, bf16[2560,320]{0,1:T(8,128)(2,1)}, u32[]{:S(2)}) copy-start(bf16[2560,320]{0,1:T(8,128)(2,1)} %param.21) | copy-start | bytes 4915204
  30.8 2.4 %copy-start.5 = (bf16[2560,96]{0,1:T(8,128)(2,1)S(1)}, bf16[2560,96]{0,1:T(8,128)(2,1)}, u32[]{:S(2)}) copy-start(bf16[2560,96]{0,1:T(8,128)(2,1)} %param.23) | copy-start | bytes 1474564
  30.8 3.5 %copy-start.6 = (bf16[2560,96]{0,1:T(8,128)(2,1)S(1)}, bf16[2560,96]{0,1:T(8,128)(2,1)}, u32[]{:S(2)}) copy-start(bf16[2560,96]{0,1:T(8,128)(2,1)} %param.26) | copy-start | bytes 1474564
  33.3 2.3 %copy-start.11 = (f32[5,2560]{1,0:T(8,128)S(1)}, f32[5,2560]{1,0:T(8,128)}, u32[]{:S(2)}) copy-start(f32[5,2560]{1,0:T(8,128)} %param.18) | copy-start | bytes 153604
  33.3 3.0 %copy-start.14 = (f32[320]{0:T(512)S(1)}, f32[320]{0:T(512)}, u32[]{:S(2)}) copy-start(f32[320]{0:T(512)} %param.22) | copy-start | bytes 3844
  33.3 3.6 %copy-start.15 = (f32[320]{0:T(512)S(1)}, f32[320]{0:T(512)}, u32[]{:S(2)}) copy-start(f32[320]{0:T(512)} %param.25) | copy-start | bytes 3844
  33.3 4.1 %copy-start.16 = (f32[320]{0:T(512)S(1)}, f32[320]{0:T(512)}, u32[]{:S(2)}) copy-start(f32[320]{0:T(512)} %param.28) | copy-start | bytes 3844
  33.3 4.7 %copy-start.17 = (f32[320]{0:T(512)S(1)}, f32[320]{0:T(512)}, u32[]{:S(2)}) copy-start(f32[320]{0:T(512)} %param.29) | copy-start | bytes 3844
  48.4 0.6 copy-start.13
  49.0 51.7 %copy-start.18 = (f32[320]{0:T(512)S(1)}, f32[320]{0:T(512)}, u32[]{:S(2)}) copy-start(f32[320]{0:T(512)} %param.30) | copy-start | bytes 3844
  49.0 52.3 %copy-start.19 = (f32[320]{0:T(512)S(1)}, f32[320]{0:T(512)}, u32[]{:S(2)}) copy-start(f32[320]{0:T(512)} %param.31) | copy-start | bytes 3844
  93.0 16.5 %all-to-all-start.1 = ((bf16[32,16,128]{2,1,0:T(8,128)(2,1)}), bf16[32,16,128]{2,1,0:T(8,128)(2,1)S(1)}, u32[]{:S(2)}, u32[]{:S(2)}) async-start(bf16[32,16,128]{2,1,0:T(8,128)(2,1)} %prefix.1), calls=%async_computation.1 | async-start | bytes 262144 | tf_op jit(solution)/shard_map/all_to_all | solution.py:340
  109.6 0.7 copy-start.4
  114.7 4.1 %collective-permute-start.9 = (bf16[128,2560]{1,0:T(8,128)(2,1)}, bf16[128,2560]{1,0:T(8,128)(2,1)S(1)}, u32[]{:S(2)}, u32[]{:S(2)}) collective-permute-start(bf16[128,2560]{1,0:T(8,128)(2,1)} %get-tuple-element.20), channel_id=1, source_target_pairs={{0,1},{1,0},{2,3},{3,2},{4,5},{5,4},{6,7},{7,6},{8,9},{9,8},{10,11... | collective-permute-start | bytes 1966088 | tf_op jit(solution)/shard_map/ppermute | solution.py:303
  118.8 0.9 copy-start.3
  122.6 7.2 %collective-permute-start.10 = (bf16[128,640]{1,0:T(8,128)(2,1)}, bf16[128,640]{1,0:T(8,128)(2,1)S(1)}, u32[]{:S(2)}, u32[]{:S(2)}) collective-permute-start(bf16[128,640]{1,0:T(8,128)(2,1)} %get-tuple-element.22), channel_id=1, source_target_pairs={{0,2},{1,3},{2,4},{3,5},{4,6},{5,7},{6,0},{7,1},{8,10},{9,11},{10,... | collective-permute-start | bytes 491528 | tf_op jit(solution)/shard_map/ppermute | solution.py:300
  122.6 10.0 %collective-permute-start.11 = (bf16[128,640]{1,0:T(8,128)(2,1)}, bf16[128,640]{1,0:T(8,128)(2,1)S(1)}, u32[]{:S(2)}, u32[]{:S(2)}) collective-permute-start(bf16[128,640]{1,0:T(8,128)(2,1)} %get-tuple-element.23), channel_id=1, source_target_pairs={{0,4},{1,5},{2,6},{3,7},{4,0},{5,1},{6,2},{7,3},{8,12},{9,13},{10,... | collective-permute-start | bytes 491528 | tf_op jit(solution)/shard_map/ppermute | solution.py:300
  124.9 8.4 %collective-permute-start.12 = (bf16[128,640]{1,0:T(8,128)(2,1)}, bf16[128,640]{1,0:T(8,128)(2,1)S(1)}, u32[]{:S(2)}, u32[]{:S(2)}) collective-permute-start(bf16[128,640]{1,0:T(8,128)(2,1)} %get-tuple-element.24), channel_id=1, source_target_pairs={{0,6},{1,7},{2,0},{3,1},{4,2},{5,3},{6,4},{7,5},{8,14},{9,15},{10,... | collective-permute-start | bytes 491528 | tf_op jit(solution)/shard_map/ppermute | solution.py:300
  129.8 3.5 %copy-start.7 = (bf16[128,640]{1,0:T(8,128)(2,1)}, bf16[128,640]{1,0:T(8,128)(2,1)S(1)}, u32[]{:S(2)}) copy-start(bf16[128,640]{1,0:T(8,128)(2,1)S(1)} %collective-permute-done.10.a_ref) | copy-start | bytes 491524
  132.6 0.7 copy-start.8
  133.3 0.7 copy-start.9
  136.0 2.6 %collective-permute-start.13 = (bf16[128,320]{1,0:T(8,128)(2,1)}, bf16[128,320]{1,0:T(8,128)(2,1)S(1)}, u32[]{:S(2)}, u32[]{:S(2)}) collective-permute-start(bf16[128,320]{1,0:T(8,128)(2,1)} %get-tuple-element.26), channel_id=1, source_target_pairs={{0,1},{1,0},{2,3},{3,2},{4,5},{5,4},{6,7},{7,6},{8,9},{9,8},{10,11... | collective-permute-start | bytes 245768 | tf_op jit(solution)/shard_map/ppermute | solution.py:303
  138.6 0.6 copy-start.10
